TPU v7x, 32 devices: a whole 2x2x4 slice. The times are simulated.
32 devices in a mesh: dp: 16 (over z, y, x), tensor: 2 (over core).
Axes of the slice: x: 2, y: 2, z: 4, core: 2. Of those that a mesh axis runs over, the one named last changes fastest.
Arguments:
- queries: bfloat16 [2048, 4096], P('dp', 'tensor'), may hold values from -4 to 4
- cached_key_rows: bfloat16 [32, 1024, 1024], P('dp', None, 'tensor'), may hold values from -1 to 1
- cached_value_rows: bfloat16 [32, 1024, 1024], P('dp', None, 'tensor'), may hold values from -6 to 6
- parent_ids: int32 [2048], P('dp'), may hold values from 0 to 31, as said below
- lengths: int32 [32], P('dp'), may hold values from 128 to 1024
- residual: bfloat16 [2048, 2048], P('dp', 'tensor'), may hold values from -4 to 4
- out_weight: bfloat16 [4096, 2048], P('tensor'), may hold values from -0.09375 to 0.09375
Outputs:
- mixed_out: bfloat16 [2048, 2048], P('dp', 'tensor')
Inputs may be any that keep to these rules, and one draw needn't show every extreme that they name: `parent_ids`: among the 128 children of one index of dp (aligned blocks), at most 16 have parents of one owner; in every draw one owner has exactly 16 children from every block.
All inputs are finite; a program needn't handle non-finite values.
Results may differ from a plain program's by a relative error of at most 0.0044.
Values may be sent and summed in bfloat16 or wider, within the bound.
A program may use at most 64 MiB of HBM per device.

v0:
```python
import functools
import math

import jax
import jax.numpy as jnp
from jax import lax
from jax.experimental import pallas as pl
from jax.experimental.pallas import tpu as pltpu
from jax.sharding import PartitionSpec as P

HEAD_WIDTH = 128


def attend(rows, key_block, value_block, prefix_length, kv_heads):
    slot_total, columns = rows.shape
    group_width = columns // (kv_heads * HEAD_WIDTH)
    prefix_span = key_block.shape[0]
    query_head_count = rows.reshape(slot_total, kv_heads, group_width, HEAD_WIDTH)
    key_heads = key_block.reshape(prefix_span, kv_heads, HEAD_WIDTH)
    value_heads = value_block.reshape(prefix_span, kv_heads, HEAD_WIDTH)
    scores = jnp.einsum(
        "sjgd,ljd->jsgl", query_head_count, key_heads, preferred_element_type=jnp.float32
    )
    scores = scores * (1.0 / math.sqrt(HEAD_WIDTH))
    live_mask = jnp.arange(prefix_span, dtype=jnp.int32) < prefix_length
    raised = jnp.where(live_mask, jnp.exp(scores), jnp.zeros((), jnp.float32))
    totals = jnp.sum(raised, axis=-1)
    summed = jnp.einsum(
        "jsgl,ljd->sjgd",
        raised.astype(jnp.bfloat16),
        value_heads,
        preferred_element_type=jnp.float32,
    )
    scaled = summed / jnp.transpose(totals, (1, 0, 2))[..., None]
    return scaled.reshape(slot_total, columns).astype(jnp.bfloat16)

PLANE = 4
MESH = pl.DeviceIdType.MESH


def exchange_kernel(
    n, out_ref, key_hbm, value_hbm, weight_hbm, length_ref, back_ref,
    landed, keys, values, weight, result, part_out, part_in,
    fetch_sem, send_sem, recv_sem, part_send, part_recv, back_send, back_recv,
):
    me = lax.axis_index("dp")
    core = lax.axis_index("tensor")
    partner = 1 - core
    planes = n // PLANE
    my_plane, my_seat = me // PLANE, me % PLANE
    capacity = out_ref.shape[1]
    parents = keys.shape[0]
    kv_heads = keys.shape[2] // HEAD_WIDTH
    columns = weight.shape[0]
    half = part_in.shape[2]
    span = keys.shape[1]
    group = columns // (kv_heads * HEAD_WIDTH)
    rows = PLANE * capacity

    fetches = [
        pltpu.make_async_copy(key_hbm, keys, fetch_sem.at[0]),
        pltpu.make_async_copy(value_hbm, values, fetch_sem.at[1]),
        pltpu.make_async_copy(weight_hbm, weight, fetch_sem.at[2]),
    ]
    for fetch in fetches:
        fetch.start()

    barrier = pltpu.get_barrier_semaphore()
    for step in range(1, n):
        pl.semaphore_signal(
            barrier, inc=1, device_id=((me + step) % n, core), device_id_type=MESH
        )
    pl.semaphore_signal(barrier, inc=1, device_id=(me, partner), device_id_type=MESH)
    pl.semaphore_wait(barrier, n)

    def query_copy(target, slot):
        return pltpu.make_async_remote_copy(
            src_ref=out_ref.at[target],
            dst_ref=landed.at[slot],
            send_sem=send_sem.at[target],
            recv_sem=recv_sem.at[slot],
            device_id=(target, core),
            device_id_type=MESH,
        )

    def back_copy(target, slot):
        return pltpu.make_async_remote_copy(
            src_ref=result.at[target],
            dst_ref=back_ref.at[slot],
            send_sem=back_send.at[target],
            recv_sem=back_recv.at[slot],
            device_id=(target, core),
            device_id_type=MESH,
        )

    def part_copy(g):
        return pltpu.make_async_remote_copy(
            src_ref=part_out.at[g],
            dst_ref=part_in.at[g],
            send_sem=part_send.at[g],
            recv_sem=part_recv.at[g],
            device_id=(me, partner),
            device_id_type=MESH,
        )

    for g in range(planes):
        for i in range(PLANE):
            if g or i:
                target = ((my_plane + g) % planes) * PLANE + (my_seat + i) % PLANE
                query_copy(target, me).start()
    landed[me] = out_ref[me]
    for fetch in fetches:
        fetch.wait()
    scale = 1.0 / math.sqrt(HEAD_WIDTH)

    @pl.loop(0, planes)
    def _(g):
        plane = (my_plane + planes - g) % planes
        seats = [plane * PLANE + (my_seat + i) % PLANE for i in range(PLANE)]

        @pl.when(g > 0)
        def _():
            query_copy(seats[0], seats[0]).wait_recv()

        for i in range(1, PLANE):
            query_copy(seats[i], seats[i]).wait_recv()

        base = plane * PLANE
        tag = landed[pl.ds(base, PLANE), :, columns:].reshape(rows, HEAD_WIDTH)
        tag = tag[:, :1].astype(jnp.float32)
        tags = jnp.concatenate([tag] * group, axis=0)
        belongs = [tags == float(p + 1) for p in range(parents)]
        limit = jnp.full(tags.shape, length_ref[parents - 1], jnp.int32)
        for p in range(parents - 1):
            limit = jnp.where(belongs[p], length_ref[p], limit)
        live = lax.broadcasted_iota(jnp.int32, (rows * group, span), 1) < limit
        pieces = []
        for j in range(kv_heads):
            at = j * HEAD_WIDTH
            q = jnp.concatenate(
                [
                    landed[
                        pl.ds(base, PLANE), :, (j * group + h) * HEAD_WIDTH:(j * group + h + 1) * HEAD_WIDTH
                    ].reshape(rows, HEAD_WIDTH)
                    for h in range(group)
                ],
                axis=0,
            )
            spread = jnp.concatenate(
                [jnp.where(belongs[p], q, jnp.zeros_like(q)) for p in range(parents)], axis=1
            )
            key_pair = jnp.concatenate(
                [keys[p, :, at:at + HEAD_WIDTH] for p in range(parents)], axis=1
            )
            scores = lax.dot_general(
                spread, key_pair, (((1,), (1,)), ((), ())), preferred_element_type=jnp.float32
            )
            raised = jnp.where(live, jnp.exp(scores * scale), 0.0)
            totals = jnp.sum(raised, axis=1, keepdims=True)
            soft = raised.astype(jnp.bfloat16)
            value_pair = jnp.concatenate(
                [values[p, :, at:at + HEAD_WIDTH] for p in range(parents)], axis=1
            )
            both = jnp.dot(soft, value_pair, preferred_element_type=jnp.float32)
            summed = both[:, (parents - 1) * HEAD_WIDTH:]
            for p in range(parents - 1):
                summed = jnp.where(
                    belongs[p], both[:, p * HEAD_WIDTH:(p + 1) * HEAD_WIDTH], summed
                )
            answer = (summed / totals).astype(jnp.bfloat16)
            pieces += [answer[h * rows:(h + 1) * rows] for h in range(group)]
        attended = jnp.concatenate(pieces, axis=1)
        theirs = pl.multiple_of(partner * half, HEAD_WIDTH)
        mine = pl.multiple_of(core * half, HEAD_WIDTH)
        part_out[g] = jnp.dot(
            attended, weight[:, pl.ds(theirs, half)], preferred_element_type=jnp.float32
        ).astype(jnp.bfloat16)
        part_copy(g).start()
        own = jnp.dot(
            attended, weight[:, pl.ds(mine, half)], preferred_element_type=jnp.float32
        )
        part_copy(g).wait_recv()
        total = (own + part_in[g].astype(jnp.float32)).astype(jnp.bfloat16)
        result[pl.ds(base, PLANE)] = total.reshape(PLANE, capacity, half)

        @pl.when(g > 0)
        def _():
            back_copy(seats[0], me).start()

        for i in range(1, PLANE):
            back_copy(seats[i], me).start()

    back_ref[me] = result[me]
    for step in range(1, n):
        other = (me + step) % n
        query_copy(other, me).wait_send()
        back_copy(other, me).wait_send()
        back_copy(other, other).wait_recv()
    for g in range(planes):
        part_copy(g).wait_send()


def exchange(n, outgoing, cached_key_rows, cached_value_rows, out_weight, lengths, half):
    _, capacity, width = outgoing.shape
    planes = n // PLANE
    whole = pl.BlockSpec(memory_space=pltpu.VMEM)
    anywhere = pl.BlockSpec(memory_space=pl.ANY)
    rows = PLANE * capacity
    dma = pltpu.SemaphoreType.DMA
    return pl.pallas_call(
        functools.partial(exchange_kernel, n),
        out_shape=jax.ShapeDtypeStruct((n, capacity, half), jnp.bfloat16),
        in_specs=[whole, anywhere, anywhere, anywhere, pl.BlockSpec(memory_space=pltpu.SMEM)],
        out_specs=whole,
        scratch_shapes=[
            pltpu.VMEM((n, capacity, width), jnp.bfloat16),
            pltpu.VMEM(cached_key_rows.shape, jnp.bfloat16),
            pltpu.VMEM(cached_value_rows.shape, jnp.bfloat16),
            pltpu.VMEM(out_weight.shape, jnp.bfloat16),
            pltpu.VMEM((n, capacity, half), jnp.bfloat16),
            pltpu.VMEM((planes, rows, half), jnp.bfloat16),
            pltpu.VMEM((planes, rows, half), jnp.bfloat16),
            dma((3,)), dma((n,)), dma((n,)), dma((planes,)), dma((planes,)), dma((n,)), dma((n,)),
        ],
        compiler_params=pltpu.CompilerParams(
            collective_id=0, has_side_effects=True, vmem_limit_bytes=56 << 20
        ),
    )(outgoing, cached_key_rows, cached_value_rows, out_weight, lengths)


def local(queries, cached_key_rows, cached_value_rows, parent_ids, lengths, residual, out_weight):
    dp_count = lax.axis_size("dp")
    children = queries.shape[0]
    columns = queries.shape[1]
    kv_heads = cached_key_rows.shape[2] // HEAD_WIDTH
    parents_here = lengths.shape[0]
    capacity = max(2, 2 * children // dp_count)
    owner_of = parent_ids // parents_here
    sub_index = parent_ids % parents_here
    slot_count = dp_count * capacity
    order_rows = jnp.arange(children, dtype=jnp.int32)
    earlier = (owner_of[:, None] == owner_of[None, :]) & (order_rows[:, None] > order_rows[None, :])
    slot_rank = jnp.sum(earlier.astype(jnp.int32), axis=1)
    slot_of = owner_of * capacity + slot_rank
    placing = jnp.arange(slot_count, dtype=jnp.int32)[:, None] == slot_of[None, :]
    placing_rows = placing.astype(jnp.bfloat16)
    tag = jnp.broadcast_to((sub_index + 1)[:, None], (children, HEAD_WIDTH)).astype(jnp.bfloat16)
    outgoing = jnp.dot(
        placing_rows,
        jnp.concatenate([queries, tag], axis=1),
        preferred_element_type=jnp.float32,
    ).astype(jnp.bfloat16)
    half = residual.shape[1]
    tensor_count = lax.axis_size("tensor")
    if capacity % 16 == 0 and dp_count % PLANE == 0 and tensor_count == 2:
        returned = exchange(
            dp_count,
            outgoing.reshape(dp_count, capacity, columns + HEAD_WIDTH),
            cached_key_rows,
            cached_value_rows,
            out_weight,
            lengths,
            half,
        ).reshape(slot_count, half)
    else:
        landed = lax.all_to_all(outgoing, "dp", split_axis=0, concat_axis=0, tiled=True)
        arrived = landed[:, :columns]
        arrived_parent = landed[:, columns].astype(jnp.int32) - 1
        answered = jnp.zeros((slot_count, columns), jnp.bfloat16)
        for parent in range(parents_here):
            answer = attend(
                arrived, cached_key_rows[parent], cached_value_rows[parent], lengths[parent], kv_heads
            )
            answered = jnp.where((arrived_parent == parent)[:, None], answer, answered)
        partial_value = jnp.dot(answered, out_weight, preferred_element_type=jnp.float32)
        mine = lax.axis_index("tensor")
        blocks = partial_value.astype(jnp.bfloat16)
        summed = lax.dynamic_slice_in_dim(blocks, mine * half, half, 1).astype(jnp.float32)
        for step in range(1, tensor_count):
            target = lax.rem(mine + step, tensor_count)
            sent = lax.dynamic_slice_in_dim(blocks, target * half, half, 1)
            ring = [(i, (i + step) % tensor_count) for i in range(tensor_count)]
            summed = summed + lax.ppermute(sent, "tensor", ring).astype(jnp.float32)
        returned = lax.all_to_all(
            summed.astype(jnp.bfloat16), "dp", split_axis=0, concat_axis=0, tiled=True
        )
    mixed = lax.dot_general(
        placing_rows, returned, (((0,), (0,)), ((), ())), preferred_element_type=jnp.float32
    )
    return (residual.astype(jnp.float32) + mixed).astype(jnp.bfloat16)


def solution(mesh):
    placed = (
        P("dp", "tensor"),
        P("dp", None, "tensor"),
        P("dp", None, "tensor"),
        P("dp"),
        P("dp"),
        P("dp", "tensor"),
        P("tensor", None),
    )
    return jax.shard_map(
        local, mesh=mesh, in_specs=placed, out_specs=P("dp", "tensor"), check_vma=False
    )
```

profile of v0, /device:TPU:0, one launch (start us, length us, event | category | flops | bytes accessed | tf_op | source)
XLA Modules:
  0.0 61.3 jit_solution(7629737337634492172)
XLA Ops:
  0.0 0.7 %and_select_fusion.1 = (s32[128]{0:T(128)S(1)}, bf16[128]{0:T(256)(128)(2,1)S(1)}) fusion(s32[128]{0:T(128)} %param.10), kind=kLoop, calls=%fused_computation.13 | loop fusion | flops 2688 | bytes 1280 | tf_op jit(solution)/shard_map/jit(floor_divide)/jit(_where)/select_n | solution.py:238
  0.7 0.2 convert_reduce_fusion
  0.9 0.1 broadcast_in_dim.2
  0.9 2.5 %convolution_convert_fusion = bf16[256,2176]{1,0:T(8,128)(2,1)} fusion(bf16[128,128]{1,0:T(8,128)(2,1)S(1)} %broadcast_in_dim.2, bf16[128,2048]{1,0:T(8,128)(2,1)} %param.7, s32[128]{0:T(128)S(1)} %multiply_add_fusion), kind=kOutput, calls=%fused_computation | convolution fusion | flops 144310272 | bytes 1671680 | tf_op jit(solution)/shard_map/dot_general | solution.py:248
  3.4 0.0 copy-start
  3.4 55.9 %shard_map.73 = bf16[16,16,1024]{2,1,0:T(8,128)(2,1)} custom-call(bf16[16,16,2176]{2,1,0:T(8,128)(2,1)} %bitcast.3, bf16[2,1024,512]{2,1,0:T(8,128)(2,1)} %key_hbm.1, bf16[2,1024,512]{2,1,0:T(8,128)(2,1)} %value_hbm.1, bf16[2048,2048]{1,0:T(8,128)(2,1)} %weight_hbm.1, s32[2]{0:T(128)} %length_ref.1), custom_call_target="tpu_custom_call" | custom-call | tf_op jit(solution)/shard_map/pallas_call | solution.py:210
  59.3 0.0 copy-done
  59.3 2.0 %fusion = bf16[128,1024]{1,0:T(8,128)(2,1)} fusion(bf16[256,1024]{1,0:T(8,128)(2,1)} %bitcast.4, bf16[128,1024]{1,0:T(8,128)(2,1)S(1)} %copy-done, s32[128]{0:T(128)S(1)} %multiply_add_fusion), kind=kOutput, calls=%fused_computation.2 | convolution fusion | flops 67534848 | bytes 1049088 | tf_op jit(solution)/shard_map/dot_general | solution.py:287
  (1 shorter events, 0.0 us)
Async XLA Ops:
  3.4 55.9 %copy-start = (bf16[128,1024]{1,0:T(8,128)(2,1)S(1)}, bf16[128,1024]{1,0:T(8,128)(2,1)}, u32[]{:S(2)}) copy-start(bf16[128,1024]{1,0:T(8,128)(2,1)} %param.12) | copy-start | bytes 786436
where the time goes:
time: 61.6 us; the launch traced here: 61.3 us
  Pallas kernels  55.9 us (91%)
  matrix products  4.49 us (7%)
  other arithmetic  0.84 us (1%)
    pallas_call x1, Pallas kernels, exchange(): pl.pallas_call(functools.partial(exchange_kernel, n), out_shape=jax.Shape...  55.9 us
    dot_general x1, matrix products, local(): jnp.dot(placing_rows, jnp.concatenate([queries, tag], axis=1), preferred_...  2.47 us
    dot_general x1, matrix products, local(): lax.dot_general(placing_rows, returned, (((0,), (0,)), ((), ())), preferr...  2.02 us

commit v1 on v0

v1 whole, which is shorter than its diff:
```python
import functools
import math

import jax
import jax.numpy as jnp
from jax import lax
from jax.experimental import pallas as pl
from jax.experimental.pallas import tpu as pltpu
from jax.sharding import PartitionSpec as P

HEAD_WIDTH = 128


def attend(rows, key_block, value_block, prefix_length, kv_heads):
    slot_total, columns = rows.shape
    group_width = columns // (kv_heads * HEAD_WIDTH)
    prefix_span = key_block.shape[0]
    query_head_count = rows.reshape(slot_total, kv_heads, group_width, HEAD_WIDTH)
    key_heads = key_block.reshape(prefix_span, kv_heads, HEAD_WIDTH)
    value_heads = value_block.reshape(prefix_span, kv_heads, HEAD_WIDTH)
    scores = jnp.einsum(
        "sjgd,ljd->jsgl", query_head_count, key_heads, preferred_element_type=jnp.float32
    )
    scores = scores * (1.0 / math.sqrt(HEAD_WIDTH))
    live_mask = jnp.arange(prefix_span, dtype=jnp.int32) < prefix_length
    raised = jnp.where(live_mask, jnp.exp(scores), jnp.zeros((), jnp.float32))
    totals = jnp.sum(raised, axis=-1)
    summed = jnp.einsum(
        "jsgl,ljd->sjgd",
        raised.astype(jnp.bfloat16),
        value_heads,
        preferred_element_type=jnp.float32,
    )
    scaled = summed / jnp.transpose(totals, (1, 0, 2))[..., None]
    return scaled.reshape(slot_total, columns).astype(jnp.bfloat16)

PLANE = 4
MESH = pl.DeviceIdType.MESH
VMEM_MB = 58


def SEND_ORDER(planes):
    return [g ^ (g >> 1) for g in range(planes)]


def flip(number, mask, bits):
    total = 0
    for bit in range(bits):
        unit = 1 << bit
        total = total + ((number // unit) % 2 + (mask // unit) % 2) % 2 * unit
    return total


def exchange_kernel(
    n, query_hbm, key_hbm, value_hbm, id_hbm, length_hbm, residual_hbm, weight_hbm, mixed_ref,
    queries, keys, values, weight, residual, lengths, ids, outgoing, landed, result, back,
    part_out, part_in, take, fetch_sem, id_send, id_recv, send_sem, recv_sem,
    part_send, part_recv, back_send, back_recv,
):
    me = lax.axis_index("dp")
    core = lax.axis_index("tensor")
    partner = 1 - core
    planes = n // PLANE
    bits = planes.bit_length() - 1
    my_plane, my_seat = me // PLANE, me % PLANE
    children, columns = queries.shape
    capacity = outgoing.shape[1]
    parents, span, _ = keys.shape
    kv_heads = keys.shape[2] // HEAD_WIDTH
    half = residual.shape[1]
    group = columns // (kv_heads * HEAD_WIDTH)
    rows = PLANE * capacity
    slots = n * capacity

    fetches = [
        pltpu.make_async_copy(source, target, fetch_sem.at[i])
        for i, (source, target) in enumerate(
            [
                (id_hbm, ids.at[me]),
                (query_hbm, queries),
                (length_hbm, lengths),
                (key_hbm, keys),
                (value_hbm, values),
                (weight_hbm, weight),
                (residual_hbm, residual),
            ]
        )
    ]
    for fetch in fetches[:2]:
        fetch.start()

    barrier = pltpu.get_barrier_semaphore()
    for step in range(1, n):
        pl.semaphore_signal(
            barrier, inc=1, device_id=((me + step) % n, core), device_id_type=MESH
        )
    pl.semaphore_signal(barrier, inc=1, device_id=(me, partner), device_id_type=MESH)
    for fetch in fetches[2:]:
        fetch.start()

    def id_copy(target, slot):
        return pltpu.make_async_remote_copy(
            src_ref=ids.at[me],
            dst_ref=ids.at[slot],
            send_sem=id_send.at[target],
            recv_sem=id_recv.at[slot],
            device_id=(target, core),
            device_id_type=MESH,
        )

    def query_copy(target, slot):
        return pltpu.make_async_remote_copy(
            src_ref=outgoing.at[target],
            dst_ref=landed.at[slot],
            send_sem=send_sem.at[target],
            recv_sem=recv_sem.at[slot],
            device_id=(target, core),
            device_id_type=MESH,
        )

    def back_copy(target, slot):
        return pltpu.make_async_remote_copy(
            src_ref=result.at[target],
            dst_ref=back.at[slot],
            send_sem=back_send.at[target],
            recv_sem=back_recv.at[slot],
            device_id=(target, core),
            device_id_type=MESH,
        )

    def part_copy(g):
        return pltpu.make_async_remote_copy(
            src_ref=part_out.at[g],
            dst_ref=part_in.at[g],
            send_sem=part_send.at[g],
            recv_sem=part_recv.at[g],
            device_id=(me, partner),
            device_id_type=MESH,
        )

    fetches[0].wait()
    square = (children, children)
    across = jnp.broadcast_to(ids[me].astype(jnp.float32), square)
    down = across.T
    owner_across = jnp.floor((across + 0.5) * (1.0 / parents))
    owner_down = jnp.floor((down + 0.5) * (1.0 / parents))
    row_at = lax.broadcasted_iota(jnp.int32, square, 0)
    column_at = lax.broadcasted_iota(jnp.int32, square, 1)
    zero, one = jnp.zeros(square, jnp.float32), jnp.ones(square, jnp.float32)
    kin = owner_across == owner_down
    alike = jnp.where(across == down, one, zero)
    lower = jnp.where(column_at < row_at, alike, zero)
    upper = jnp.where(row_at < column_at, alike, zero)
    before_down = jnp.where(kin, jnp.where(across < down, one, lower), zero)
    before_across = jnp.where(kin, jnp.where(down < across, one, upper), zero)
    slot_down = owner_down[:, :1] * capacity + jnp.sum(before_down, axis=1, keepdims=True)
    slot_across = owner_across[:1] * capacity + jnp.sum(before_across, axis=0, keepdims=True)
    place = jnp.where(
        lax.broadcasted_iota(jnp.int32, (slots, children), 0).astype(jnp.float32) == slot_across,
        jnp.ones((slots, children), jnp.float32),
        jnp.zeros((slots, children), jnp.float32),
    ).astype(jnp.bfloat16)
    take[...] = jnp.where(
        lax.broadcasted_iota(jnp.int32, (children, slots), 1).astype(jnp.float32) == slot_down,
        jnp.ones((children, slots), jnp.float32),
        jnp.zeros((children, slots), jnp.float32),
    ).astype(jnp.bfloat16)
    fetches[1].wait()
    outgoing[...] = (
        jnp.dot(place, queries[...], preferred_element_type=jnp.float32)
        .astype(jnp.bfloat16)
        .reshape(n, capacity, columns)
    )
    pl.semaphore_wait(barrier, n)

    for step in range(1, n):
        id_copy((me + step) % n, me).start()
    for mask in SEND_ORDER(planes):
        for i in range(PLANE):
            if mask or i:
                target = flip(my_plane, mask, bits) * PLANE + flip(my_seat, i, 2)
                query_copy(target, me).start()
    landed[me] = outgoing[me]
    for fetch in fetches[2:]:
        fetch.wait()
    for step in range(1, n):
        other = (me + step) % n
        id_copy(other, other).wait_recv()
    scale = math.log2(math.e) / math.sqrt(HEAD_WIDTH)

    @pl.loop(0, planes)
    def _(g):
        mask = flip(g, g // 2, bits)
        plane = flip(my_plane, mask, bits)
        seats = [plane * PLANE + flip(my_seat, i, 2) for i in range(PLANE)]

        @pl.when(g > 0)
        def _():
            query_copy(seats[0], seats[0]).wait_recv()

        for i in range(1, PLANE):
            query_copy(seats[i], seats[i]).wait_recv()

        base = plane * PLANE
        spot = lax.broadcasted_iota(jnp.int32, (capacity, 1), 0).astype(jnp.float32)
        tag_parts = []
        for i in range(PLANE):
            known = ids[base + i]
            number = jnp.zeros((capacity, 1), jnp.float32)
            for p in range(parents - 1):
                smaller = jnp.where(
                    known >= me * parents, jnp.where(known <= me * parents + p, 1.0, 0.0), 0.0
                )
                count = jnp.sum(smaller, axis=1, keepdims=True)
                number = number + jnp.where(spot >= count, 1.0, 0.0)
            tag_parts.append(number)
        tags = jnp.concatenate(tag_parts * group, axis=0)
        belongs = [tags == float(p) for p in range(parents)]
        limit = jnp.full(tags.shape, lengths[parents - 1], jnp.int32)
        for p in range(parents - 1):
            limit = jnp.where(belongs[p], lengths[p], limit)
        live = lax.broadcasted_iota(jnp.int32, (rows * group, span), 1) < limit
        pieces = []
        for j in range(kv_heads):
            at = j * HEAD_WIDTH
            q = jnp.concatenate(
                [
                    landed[
                        pl.ds(base, PLANE), :, (j * group + h) * HEAD_WIDTH:(j * group + h + 1) * HEAD_WIDTH
                    ].reshape(rows, HEAD_WIDTH)
                    for h in range(group)
                ],
                axis=0,
            )
            spread = jnp.concatenate(
                [jnp.where(belongs[p], q, jnp.zeros_like(q)) for p in range(parents)], axis=1
            )
            key_pair = jnp.concatenate(
                [keys[p, :, at:at + HEAD_WIDTH] for p in range(parents)], axis=1
            )
            scores = lax.dot_general(
                spread, key_pair, (((1,), (1,)), ((), ())), preferred_element_type=jnp.float32
            )
            raised = jnp.where(live, jnp.exp2(scores * scale), 0.0)
            totals = jnp.sum(raised, axis=1, keepdims=True)
            soft = raised.astype(jnp.bfloat16)
            value_pair = jnp.concatenate(
                [values[p, :, at:at + HEAD_WIDTH] for p in range(parents)], axis=1
            )
            both = jnp.dot(soft, value_pair, preferred_element_type=jnp.float32)
            summed = both[:, (parents - 1) * HEAD_WIDTH:]
            for p in range(parents - 1):
                summed = jnp.where(
                    belongs[p], both[:, p * HEAD_WIDTH:(p + 1) * HEAD_WIDTH], summed
                )
            answer = (summed / totals).astype(jnp.bfloat16)
            pieces += [answer[h * rows:(h + 1) * rows] for h in range(group)]
        attended = jnp.concatenate(pieces, axis=1)
        theirs = pl.multiple_of(partner * half, HEAD_WIDTH)
        mine = pl.multiple_of(core * half, HEAD_WIDTH)
        part_out[g] = jnp.dot(
            attended, weight[:, pl.ds(theirs, half)], preferred_element_type=jnp.float32
        ).astype(jnp.bfloat16)
        part_copy(g).start()
        own = jnp.dot(
            attended, weight[:, pl.ds(mine, half)], preferred_element_type=jnp.float32
        )
        part_copy(g).wait_recv()
        total = (own + part_in[g].astype(jnp.float32)).astype(jnp.bfloat16)
        result[pl.ds(base, PLANE)] = total.reshape(PLANE, capacity, half)

        @pl.when(g > 0)
        def _():
            back_copy(seats[0], me).start()

        for i in range(1, PLANE):
            back_copy(seats[i], me).start()

    back[me] = result[me]
    for step in range(1, n):
        other = (me + step) % n
        id_copy(other, me).wait_send()
        query_copy(other, me).wait_send()
        back_copy(other, me).wait_send()
        back_copy(other, other).wait_recv()
    for g in range(planes):
        part_copy(g).wait_send()
    mixed = jnp.dot(
        take[...], back[...].reshape(slots, half), preferred_element_type=jnp.float32
    )
    mixed_ref[...] = (residual[...].astype(jnp.float32) + mixed).astype(jnp.bfloat16)


def exchange(n, capacity, queries, cached_key_rows, cached_value_rows, parent_ids, lengths, residual, out_weight):
    children, columns = queries.shape
    half = residual.shape[1]
    planes = n // PLANE
    anywhere = pl.BlockSpec(memory_space=pltpu.HBM)
    rows = PLANE * capacity
    dma = pltpu.SemaphoreType.DMA

    def held(*shape):
        return pltpu.VMEM(shape, jnp.bfloat16)

    return pl.pallas_call(
        functools.partial(exchange_kernel, n),
        out_shape=jax.ShapeDtypeStruct(residual.shape, jnp.bfloat16),
        in_specs=[anywhere] * 7,
        out_specs=pl.BlockSpec(memory_space=pltpu.VMEM),
        scratch_shapes=[
            held(*queries.shape),
            held(*cached_key_rows.shape),
            held(*cached_value_rows.shape),
            held(*out_weight.shape),
            held(*residual.shape),
            pltpu.SMEM(lengths.shape, jnp.int32),
            pltpu.VMEM((n, 1, children), jnp.int32),
            held(n, capacity, columns),
            held(n, capacity, columns),
            held(n, capacity, half),
            held(n, capacity, half),
            held(planes, rows, half),
            held(planes, rows, half),
            held(children, n * capacity),
            dma((7,)), dma((n,)), dma((n,)), dma((n,)), dma((n,)),
            dma((planes,)), dma((planes,)), dma((n,)), dma((n,)),
        ],
        compiler_params=pltpu.CompilerParams(
            collective_id=0, has_side_effects=True, vmem_limit_bytes=VMEM_MB << 20
        ),
    )(queries, cached_key_rows, cached_value_rows, parent_ids.reshape(1, children), lengths, residual, out_weight)


def local(queries, cached_key_rows, cached_value_rows, parent_ids, lengths, residual, out_weight):
    dp_count = lax.axis_size("dp")
    children = queries.shape[0]
    columns = queries.shape[1]
    kv_heads = cached_key_rows.shape[2] // HEAD_WIDTH
    parents_here = lengths.shape[0]
    capacity = max(2, 2 * children // dp_count)
    half = residual.shape[1]
    tensor_count = lax.axis_size("tensor")
    planes = dp_count // PLANE
    if (
        capacity % 16 == 0
        and children % 128 == 0
        and dp_count % PLANE == 0
        and planes & (planes - 1) == 0
        and tensor_count == 2
    ):
        return exchange(
            dp_count, capacity, queries, cached_key_rows, cached_value_rows, parent_ids, lengths, residual, out_weight
        )
    owner_of = parent_ids // parents_here
    sub_index = parent_ids % parents_here
    slot_count = dp_count * capacity
    order_rows = jnp.arange(children, dtype=jnp.int32)
    earlier = (owner_of[:, None] == owner_of[None, :]) & (order_rows[:, None] > order_rows[None, :])
    slot_rank = jnp.sum(earlier.astype(jnp.int32), axis=1)
    slot_of = owner_of * capacity + slot_rank
    placing = jnp.arange(slot_count, dtype=jnp.int32)[:, None] == slot_of[None, :]
    placing_rows = placing.astype(jnp.bfloat16)
    tag = jnp.broadcast_to((sub_index + 1)[:, None], (children, HEAD_WIDTH)).astype(jnp.bfloat16)
    outgoing = jnp.dot(
        placing_rows,
        jnp.concatenate([queries, tag], axis=1),
        preferred_element_type=jnp.float32,
    ).astype(jnp.bfloat16)
    landed = lax.all_to_all(outgoing, "dp", split_axis=0, concat_axis=0, tiled=True)
    arrived = landed[:, :columns]
    arrived_parent = landed[:, columns].astype(jnp.int32) - 1
    answered = jnp.zeros((slot_count, columns), jnp.bfloat16)
    for parent in range(parents_here):
        answer = attend(
            arrived, cached_key_rows[parent], cached_value_rows[parent], lengths[parent], kv_heads
        )
        answered = jnp.where((arrived_parent == parent)[:, None], answer, answered)
    partial_value = jnp.dot(answered, out_weight, preferred_element_type=jnp.float32)
    mine = lax.axis_index("tensor")
    blocks = partial_value.astype(jnp.bfloat16)
    summed = lax.dynamic_slice_in_dim(blocks, mine * half, half, 1).astype(jnp.float32)
    for step in range(1, tensor_count):
        target = lax.rem(mine + step, tensor_count)
        sent = lax.dynamic_slice_in_dim(blocks, target * half, half, 1)
        ring = [(i, (i + step) % tensor_count) for i in range(tensor_count)]
        summed = summed + lax.ppermute(sent, "tensor", ring).astype(jnp.float32)
    returned = lax.all_to_all(
        summed.astype(jnp.bfloat16), "dp", split_axis=0, concat_axis=0, tiled=True
    )
    mixed = lax.dot_general(
        placing_rows, returned, (((0,), (0,)), ((), ())), preferred_element_type=jnp.float32
    )
    return (residual.astype(jnp.float32) + mixed).astype(jnp.bfloat16)


def solution(mesh):
    placed = (
        P("dp", "tensor"),
        P("dp", None, "tensor"),
        P("dp", None, "tensor"),
        P("dp"),
        P("dp"),
        P("dp", "tensor"),
        P("tensor", None),
    )
    return jax.shard_map(
        local, mesh=mesh, in_specs=placed, out_specs=P("dp", "tensor"), check_vma=False
    )
```

time: 61.6 us -> 48 us (0.78)
  the two profiles are of different devices: /device:TPU:0 before, /device:TPU:8 now
where the time goes in v1:
time: 48 us; the launch traced here: 47.5 us
  Pallas kernels  45.8 us (95%)
  local copies, waits for them, and re-layouts  1.67 us (3%)
    pallas_call x1, Pallas kernels, exchange(): pl.pallas_call(functools.partial(exchange_kernel, n), out_shape=jax.Shape...  45.8 us
    unnamed x1, local copies, waits for them, and re-layouts  1.67 us

profile of v1, /device:TPU:8, one launch (start us, length us, event | category | flops | bytes accessed | tf_op | source)
XLA Modules:
  0.0 47.5 jit_solution(2908540108861192610)
XLA Ops:
  0.0 45.8 %shard_map.73 = bf16[128,1024]{1,0:T(8,128)(2,1)} custom-call(bf16[128,2048]{1,0:T(8,128)(2,1)} %query_hbm.1, bf16[2,1024,512]{2,1,0:T(8,128)(2,1)} %key_hbm.1, bf16[2,1024,512]{2,1,0:T(8,128)(2,1)} %value_hbm.1, s32[1,128]{1,0:T(1,128)} %bitcast.1, s32[2]{0:T(128)} %length_hbm.1, bf16[128,1024]{1,0:T(8,128)(2,1)} %residual_hbm.1, bf16[2048,2048]{1,0:T(8,128)(2,1)} %weight_hbm.1), custom_call_target="tpu_custom_call" | custom-call | tf_op jit(solution)/shard_map/pallas_call | solution.py:305
  45.8 1.7 %copy.9 = bf16[128,1024]{1,0:T(8,128)(2,1)} copy(bf16[128,1024]{1,0:T(8,128)(2,1)} %shard_map.73) | data formatting | bytes 524288

commit v2 on v1

--- a/solution.py
+++ b/solution.py
@@ -36,11 +36,18 @@
 
 PLANE = 4
 MESH = pl.DeviceIdType.MESH
-VMEM_MB = 58
-
-
-def SEND_ORDER(planes):
-    return [g ^ (g >> 1) for g in range(planes)]
+VMEM_MB = 40
+
+
+SENDS = [(0, 0, 0), (0, 0, 1), (0, 0, 2), (0, 0, 3), (1, 1, 0), (1, 1, 1), (1, 1, 2), (1, 1, 3), (2, 2, 0), (2, 2, 1), (2, 2, 2), (2, 2, 3), (3, 3, 0), (3, 3, 1), (3, 3, 2), (3, 3, 3)]
+STEP_OUTER, STEP_INNER = (0, 1, 3, 2), (0, 1, 2, 3)
+
+
+def pick(outer, inner, at_inner, step):
+    return sum(
+        (o + at_inner * (i - o)) * jnp.where(step == k, 1, 0)
+        for k, (o, i) in enumerate(zip(outer, inner))
+    )
 
 
 def flip(number, mask, bits):
@@ -52,8 +59,8 @@
 
 
 def exchange_kernel(
-    n, query_hbm, key_hbm, value_hbm, id_hbm, length_hbm, residual_hbm, weight_hbm, mixed_ref,
-    queries, keys, values, weight, residual, lengths, ids, outgoing, landed, result, back,
+    n, query_hbm, key_hbm, value_hbm, id_hbm, length_hbm, weight_hbm, mixed_ref,
+    queries, keys, values, weight, lengths, ids, outgoing, landed, result, back,
     part_out, part_in, take, fetch_sem, id_send, id_recv, send_sem, recv_sem,
     part_send, part_recv, back_send, back_recv,
 ):
@@ -67,7 +74,7 @@
     capacity = outgoing.shape[1]
     parents, span, _ = keys.shape
     kv_heads = keys.shape[2] // HEAD_WIDTH
-    half = residual.shape[1]
+    half = result.shape[2]
     group = columns // (kv_heads * HEAD_WIDTH)
     rows = PLANE * capacity
     slots = n * capacity
@@ -82,7 +89,6 @@
                 (key_hbm, keys),
                 (value_hbm, values),
                 (weight_hbm, weight),
-                (residual_hbm, residual),
             ]
         )
     ]
@@ -95,9 +101,6 @@
             barrier, inc=1, device_id=((me + step) % n, core), device_id_type=MESH
         )
     pl.semaphore_signal(barrier, inc=1, device_id=(me, partner), device_id_type=MESH)
-    for fetch in fetches[2:]:
-        fetch.start()
-
     def id_copy(target, slot):
         return pltpu.make_async_remote_copy(
             src_ref=ids.at[me],
@@ -160,26 +163,34 @@
         jnp.ones((slots, children), jnp.float32),
         jnp.zeros((slots, children), jnp.float32),
     ).astype(jnp.bfloat16)
+    fetches[1].wait()
+    for fetch in fetches[2:]:
+        fetch.start()
+    outgoing[...] = (
+        jnp.dot(place, queries[...], preferred_element_type=jnp.float32)
+        .astype(jnp.bfloat16)
+        .reshape(n, capacity, columns)
+    )
+    pl.semaphore_wait(barrier, n)
+
+    for step in range(1, n):
+        id_copy((me + step) % n, me).start()
+    at_inner = (my_plane + 1) // 2 % 2
+    for o, inner, i in SENDS:
+        mask = o + at_inner * (inner - o)
+        target = flip(my_plane, mask, bits) * PLANE + flip(my_seat, i, 2)
+        if i == 0 and 0 in (o, inner):
+
+            @pl.when(mask > 0)
+            def _(target=target):
+                query_copy(target, me).start()
+        else:
+            query_copy(target, me).start()
     take[...] = jnp.where(
         lax.broadcasted_iota(jnp.int32, (children, slots), 1).astype(jnp.float32) == slot_down,
         jnp.ones((children, slots), jnp.float32),
         jnp.zeros((children, slots), jnp.float32),
     ).astype(jnp.bfloat16)
-    fetches[1].wait()
-    outgoing[...] = (
-        jnp.dot(place, queries[...], preferred_element_type=jnp.float32)
-        .astype(jnp.bfloat16)
-        .reshape(n, capacity, columns)
-    )
-    pl.semaphore_wait(barrier, n)
-
-    for step in range(1, n):
-        id_copy((me + step) % n, me).start()
-    for mask in SEND_ORDER(planes):
-        for i in range(PLANE):
-            if mask or i:
-                target = flip(my_plane, mask, bits) * PLANE + flip(my_seat, i, 2)
-                query_copy(target, me).start()
     landed[me] = outgoing[me]
     for fetch in fetches[2:]:
         fetch.wait()
@@ -190,11 +201,11 @@
 
     @pl.loop(0, planes)
     def _(g):
-        mask = flip(g, g // 2, bits)
+        mask = pick(STEP_OUTER, STEP_INNER, at_inner, g)
         plane = flip(my_plane, mask, bits)
         seats = [plane * PLANE + flip(my_seat, i, 2) for i in range(PLANE)]
 
-        @pl.when(g > 0)
+        @pl.when(mask > 0)
         def _():
             query_copy(seats[0], seats[0]).wait_recv()
 
@@ -269,7 +280,7 @@
         total = (own + part_in[g].astype(jnp.float32)).astype(jnp.bfloat16)
         result[pl.ds(base, PLANE)] = total.reshape(PLANE, capacity, half)
 
-        @pl.when(g > 0)
+        @pl.when(mask > 0)
         def _():
             back_copy(seats[0], me).start()
 
@@ -277,18 +288,20 @@
             back_copy(seats[i], me).start()
 
     back[me] = result[me]
+    for step in range(1, n):
+        other = (me + step) % n
+        back_copy(other, other).wait_recv()
+    mixed = jnp.dot(
+        take[...], back[...].reshape(slots, half), preferred_element_type=jnp.float32
+    )
+    mixed_ref[...] = mixed.astype(jnp.bfloat16)
     for step in range(1, n):
         other = (me + step) % n
         id_copy(other, me).wait_send()
         query_copy(other, me).wait_send()
         back_copy(other, me).wait_send()
-        back_copy(other, other).wait_recv()
     for g in range(planes):
         part_copy(g).wait_send()
-    mixed = jnp.dot(
-        take[...], back[...].reshape(slots, half), preferred_element_type=jnp.float32
-    )
-    mixed_ref[...] = (residual[...].astype(jnp.float32) + mixed).astype(jnp.bfloat16)
 
 
 def exchange(n, capacity, queries, cached_key_rows, cached_value_rows, parent_ids, lengths, residual, out_weight):
@@ -305,14 +318,13 @@
     return pl.pallas_call(
         functools.partial(exchange_kernel, n),
         out_shape=jax.ShapeDtypeStruct(residual.shape, jnp.bfloat16),
-        in_specs=[anywhere] * 7,
+        in_specs=[anywhere] * 6,
         out_specs=pl.BlockSpec(memory_space=pltpu.VMEM),
         scratch_shapes=[
             held(*queries.shape),
             held(*cached_key_rows.shape),
             held(*cached_value_rows.shape),
             held(*out_weight.shape),
-            held(*residual.shape),
             pltpu.SMEM(lengths.shape, jnp.int32),
             pltpu.VMEM((n, 1, children), jnp.int32),
             held(n, capacity, columns),
@@ -322,13 +334,25 @@
             held(planes, rows, half),
             held(planes, rows, half),
             held(children, n * capacity),
-            dma((7,)), dma((n,)), dma((n,)), dma((n,)), dma((n,)),
+            dma((6,)), dma((n,)), dma((n,)), dma((n,)), dma((n,)),
             dma((planes,)), dma((planes,)), dma((n,)), dma((n,)),
         ],
         compiler_params=pltpu.CompilerParams(
             collective_id=0, has_side_effects=True, vmem_limit_bytes=VMEM_MB << 20
         ),
-    )(queries, cached_key_rows, cached_value_rows, parent_ids.reshape(1, children), lengths, residual, out_weight)
+    )(
+        *(
+            pltpu.with_memory_space_constraint(operand, pltpu.HBM)
+            for operand in (
+                queries,
+                cached_key_rows,
+                cached_value_rows,
+                parent_ids.reshape(1, children),
+                lengths,
+                out_weight,
+            )
+        )
+    )
 
 
 def local(queries, cached_key_rows, cached_value_rows, parent_ids, lengths, residual, out_weight):
@@ -348,9 +372,10 @@
         and planes & (planes - 1) == 0
         and tensor_count == 2
     ):
-        return exchange(
+        mixed = exchange(
             dp_count, capacity, queries, cached_key_rows, cached_value_rows, parent_ids, lengths, residual, out_weight
         )
+        return (residual.astype(jnp.float32) + mixed.astype(jnp.float32)).astype(jnp.bfloat16)
     owner_of = parent_ids // parents_here
     sub_index = parent_ids % parents_here
     slot_count = dp_count * capacity

time: 48 us -> 44.2 us (0.921)
  Pallas kernels: 45.8 us -> 42.9 us
  local copies, waits for them, and re-layouts: 1.67 us -> 0.01 us
  other arithmetic: 0 us -> 0.77 us
    pallas_call x1, Pallas kernels: 45.8 us -> 42.9 us  [exchange(): pl.pallas_call(functools.partial(exchange_kernel, n), out_shape=jax.Shape...]
    unnamed x1 -> x2, local copies, waits for them, and re-layouts: 1.67 us -> 0.01 us
    convert_element_type x0 -> x1, other arithmetic: none -> 0.77 us  [local(): (residual.astype(jnp.float32) + mixed.astype(jnp.float32)).astype(jnp.bfl...]
where the time goes in v2:
time: 44.2 us; the launch traced here: 43.7 us
  Pallas kernels  42.9 us (97%)
  other arithmetic  0.77 us (2%)
    pallas_call x1, Pallas kernels, exchange(): pl.pallas_call(functools.partial(exchange_kernel, n), out_shape=jax.Shape...  42.9 us

profile of v2, /device:TPU:8, one launch (start us, length us, event | category | flops | bytes accessed | tf_op | source)
XLA Modules:
  0.0 43.7 jit_solution(13580724697119251077)
XLA Ops:
  0.0 0.0 copy-start
  0.0 42.9 %shard_map.73 = bf16[128,1024]{1,0:T(8,128)(2,1)S(1)} custom-call(bf16[128,2048]{1,0:T(8,128)(2,1)} %query_hbm.1, bf16[2,1024,512]{2,1,0:T(8,128)(2,1)} %key_hbm.1, bf16[2,1024,512]{2,1,0:T(8,128)(2,1)} %value_hbm.1, s32[1,128]{1,0:T(1,128)} %bitcast.1, s32[2]{0:T(128)} %length_hbm.1, bf16[2048,2048]{1,0:T(8,128)(2,1)} %weight_hbm.1), custom_call_target="tpu_custom_call" | custom-call | tf_op jit(solution)/shard_map/pallas_call | solution.py:318
  43.0 0.0 copy-done
  43.0 0.8 %add_convert_fusion = bf16[128,1024]{1,0:T(8,128)(2,1)} fusion(bf16[128,1024]{1,0:T(8,128)(2,1)S(1)} %shard_map.73, bf16[128,1024]{1,0:T(8,128)(2,1)S(1)} %copy-done), kind=kLoop, calls=%fused_computation | loop fusion | flops 524288 | bytes 786432 | tf_op jit(solution)/shard_map/convert_element_type | solution.py:378
Async XLA Ops:
  0.0 43.0 %copy-start = (bf16[128,1024]{1,0:T(8,128)(2,1)S(1)}, bf16[128,1024]{1,0:T(8,128)(2,1)}, u32[]{:S(2)}) copy-start(bf16[128,1024]{1,0:T(8,128)(2,1)} %param.12) | copy-start | bytes 786436

commit v3 on v2

--- a/solution.py
+++ b/solution.py
@@ -39,7 +39,7 @@
 VMEM_MB = 40
 
 
-SENDS = [(0, 0, 0), (0, 0, 1), (0, 0, 2), (0, 0, 3), (1, 1, 0), (1, 1, 1), (1, 1, 2), (1, 1, 3), (2, 2, 0), (2, 2, 1), (2, 2, 2), (2, 2, 3), (3, 3, 0), (3, 3, 1), (3, 3, 2), (3, 3, 3)]
+FIRST, SECOND, OUTER = (0, 3), (1, 2), (0, 1, 2, 3)
 STEP_OUTER, STEP_INNER = (0, 1, 3, 2), (0, 1, 2, 3)
 
 
@@ -61,7 +61,7 @@
 def exchange_kernel(
     n, query_hbm, key_hbm, value_hbm, id_hbm, length_hbm, weight_hbm, mixed_ref,
     queries, keys, values, weight, lengths, ids, outgoing, landed, result, back,
-    part_out, part_in, take, fetch_sem, id_send, id_recv, send_sem, recv_sem,
+    part_out, part_in, own, take, fetch_sem, id_send, id_recv, send_sem, recv_sem,
     part_send, part_recv, back_send, back_recv,
 ):
     me = lax.axis_index("dp")
@@ -96,10 +96,16 @@
         fetch.start()
 
     barrier = pltpu.get_barrier_semaphore()
-    for step in range(1, n):
-        pl.semaphore_signal(
-            barrier, inc=1, device_id=((me + step) % n, core), device_id_type=MESH
-        )
+    at_inner = (my_plane + 1) // 2 % 2
+
+    def greet(mask):
+        for i in range(PLANE):
+            target = flip(my_plane, mask, bits) * PLANE + flip(my_seat, i, 2)
+            if mask or i:
+                pl.semaphore_signal(barrier, inc=1, device_id=(target, core), device_id_type=MESH)
+
+    for mask in FIRST:
+        greet(mask)
     pl.semaphore_signal(barrier, inc=1, device_id=(me, partner), device_id_type=MESH)
     def id_copy(target, slot):
         return pltpu.make_async_remote_copy(
@@ -171,21 +177,34 @@
         .astype(jnp.bfloat16)
         .reshape(n, capacity, columns)
     )
-    pl.semaphore_wait(barrier, n)
-
-    for step in range(1, n):
-        id_copy((me + step) % n, me).start()
-    at_inner = (my_plane + 1) // 2 % 2
-    for o, inner, i in SENDS:
-        mask = o + at_inner * (inner - o)
-        target = flip(my_plane, mask, bits) * PLANE + flip(my_seat, i, 2)
-        if i == 0 and 0 in (o, inner):
-
-            @pl.when(mask > 0)
-            def _(target=target):
-                query_copy(target, me).start()
-        else:
-            query_copy(target, me).start()
+    def send(masks):
+        for mask in masks:
+            for i in range(PLANE):
+                target = flip(my_plane, mask, bits) * PLANE + flip(my_seat, i, 2)
+                if mask or i:
+                    id_copy(target, me).start()
+        for mask in masks:
+            for i in range(PLANE):
+                target = flip(my_plane, mask, bits) * PLANE + flip(my_seat, i, 2)
+                if mask or i:
+                    query_copy(target, me).start()
+
+    @pl.when(at_inner == 1)
+    def _():
+        pl.semaphore_wait(barrier, n // 2)
+        for mask in SECOND:
+            greet(mask)
+        send(FIRST)
+        pl.semaphore_wait(barrier, n // 2)
+        send(SECOND)
+
+    @pl.when(at_inner == 0)
+    def _():
+        pl.semaphore_wait(barrier, n)
+        for mask in SECOND:
+            greet(mask)
+        send(OUTER)
+
     take[...] = jnp.where(
         lax.broadcasted_iota(jnp.int32, (children, slots), 1).astype(jnp.float32) == slot_down,
         jnp.ones((children, slots), jnp.float32),
@@ -273,11 +292,11 @@
             attended, weight[:, pl.ds(theirs, half)], preferred_element_type=jnp.float32
         ).astype(jnp.bfloat16)
         part_copy(g).start()
-        own = jnp.dot(
+        own[...] = jnp.dot(
             attended, weight[:, pl.ds(mine, half)], preferred_element_type=jnp.float32
         )
         part_copy(g).wait_recv()
-        total = (own + part_in[g].astype(jnp.float32)).astype(jnp.bfloat16)
+        total = (own[...] + part_in[g].astype(jnp.float32)).astype(jnp.bfloat16)
         result[pl.ds(base, PLANE)] = total.reshape(PLANE, capacity, half)
 
         @pl.when(mask > 0)
@@ -288,6 +307,12 @@
             back_copy(seats[i], me).start()
 
     back[me] = result[me]
+    for step in range(1, n):
+        other = (me + step) % n
+        id_copy(other, me).wait_send()
+        query_copy(other, me).wait_send()
+    for g in range(planes):
+        part_copy(g).wait_send()
     for step in range(1, n):
         other = (me + step) % n
         back_copy(other, other).wait_recv()
@@ -296,12 +321,7 @@
     )
     mixed_ref[...] = mixed.astype(jnp.bfloat16)
     for step in range(1, n):
-        other = (me + step) % n
-        id_copy(other, me).wait_send()
-        query_copy(other, me).wait_send()
-        back_copy(other, me).wait_send()
-    for g in range(planes):
-        part_copy(g).wait_send()
+        back_copy((me + step) % n, me).wait_send()
 
 
 def exchange(n, capacity, queries, cached_key_rows, cached_value_rows, parent_ids, lengths, residual, out_weight):
@@ -333,6 +353,7 @@
             held(n, capacity, half),
             held(planes, rows, half),
             held(planes, rows, half),
+            pltpu.VMEM((rows, half), jnp.float32),
             held(children, n * capacity),
             dma((6,)), dma((n,)), dma((n,)), dma((n,)), dma((n,)),
             dma((planes,)), dma((planes,)), dma((n,)), dma((n,)),
@@ -369,7 +390,7 @@
         capacity % 16 == 0
         and children % 128 == 0
         and dp_count % PLANE == 0
-        and planes & (planes - 1) == 0
+        and planes == len(SECOND + FIRST)
         and tensor_count == 2
     ):
         mixed = exchange(

time: 44.2 us -> 41.8 us (0.946)
  Pallas kernels: 42.9 us -> 40.9 us
    pallas_call x1, Pallas kernels: 42.9 us -> 40.9 us  [exchange(): pl.pallas_call(functools.partial(exchange_kernel, n), out_shape=jax.Shape...]
where the time goes in v3:
time: 41.8 us; the launch traced here: 41.7 us
  Pallas kernels  40.9 us (98%)
  other arithmetic  0.77 us (2%)
    pallas_call x1, Pallas kernels, exchange(): pl.pallas_call(functools.partial(exchange_kernel, n), out_shape=jax.Shape...  40.9 us

profile of v3, /device:TPU:8, one launch (start us, length us, event | category | flops | bytes accessed | tf_op | source)
XLA Modules:
  0.0 41.7 jit_solution(7708037390643518249)
XLA Ops:
  0.0 0.0 copy-start
  0.0 40.9 %shard_map.73 = bf16[128,1024]{1,0:T(8,128)(2,1)S(1)} custom-call(bf16[128,2048]{1,0:T(8,128)(2,1)} %query_hbm.1, bf16[2,1024,512]{2,1,0:T(8,128)(2,1)} %key_hbm.1, bf16[2,1024,512]{2,1,0:T(8,128)(2,1)} %value_hbm.1, s32[1,128]{1,0:T(1,128)} %bitcast.1, s32[2]{0:T(128)} %length_hbm.1, bf16[2048,2048]{1,0:T(8,128)(2,1)} %weight_hbm.1), custom_call_target="tpu_custom_call" | custom-call | tf_op jit(solution)/shard_map/pallas_call | solution.py:338
  40.9 0.0 copy-done
  40.9 0.8 %add_convert_fusion = bf16[128,1024]{1,0:T(8,128)(2,1)} fusion(bf16[128,1024]{1,0:T(8,128)(2,1)S(1)} %shard_map.73, bf16[128,1024]{1,0:T(8,128)(2,1)S(1)} %copy-done), kind=kLoop, calls=%fused_computation | loop fusion | flops 524288 | bytes 786432 | tf_op jit(solution)/shard_map/convert_element_type | solution.py:399
Async XLA Ops:
  0.0 40.9 %copy-start = (bf16[128,1024]{1,0:T(8,128)(2,1)S(1)}, bf16[128,1024]{1,0:T(8,128)(2,1)}, u32[]{:S(2)}) copy-start(bf16[128,1024]{1,0:T(8,128)(2,1)} %param.12) | copy-start | bytes 786436

commit v4 on v3

--- a/solution.py
+++ b/solution.py
@@ -107,44 +107,35 @@
     for mask in FIRST:
         greet(mask)
     pl.semaphore_signal(barrier, inc=1, device_id=(me, partner), device_id_type=MESH)
-    def id_copy(target, slot):
+    def remote(source, target, send, recv, device):
         return pltpu.make_async_remote_copy(
-            src_ref=ids.at[me],
-            dst_ref=ids.at[slot],
-            send_sem=id_send.at[target],
-            recv_sem=id_recv.at[slot],
-            device_id=(target, core),
+            src_ref=source,
+            dst_ref=target,
+            send_sem=send,
+            recv_sem=recv,
+            device_id=device,
             device_id_type=MESH,
         )
 
-    def query_copy(target, slot):
-        return pltpu.make_async_remote_copy(
-            src_ref=outgoing.at[target],
-            dst_ref=landed.at[slot],
-            send_sem=send_sem.at[target],
-            recv_sem=recv_sem.at[slot],
-            device_id=(target, core),
-            device_id_type=MESH,
-        )
-
-    def back_copy(target, slot):
-        return pltpu.make_async_remote_copy(
-            src_ref=result.at[target],
-            dst_ref=back.at[slot],
-            send_sem=back_send.at[target],
-            recv_sem=back_recv.at[slot],
-            device_id=(target, core),
-            device_id_type=MESH,
-        )
+    def id_copy(target):
+        return remote(ids.at[me], ids.at[me], id_send, id_recv, (target, core))
+
+    def query_copy(target, mask):
+        return remote(
+            outgoing.at[target], landed.at[me], send_sem, recv_sem.at[mask], (target, core)
+        )
+
+    def back_copy(target):
+        return remote(result.at[target], back.at[me], back_send, back_recv, (target, core))
 
     def part_copy(g):
-        return pltpu.make_async_remote_copy(
-            src_ref=part_out.at[g],
-            dst_ref=part_in.at[g],
-            send_sem=part_send.at[g],
-            recv_sem=part_recv.at[g],
-            device_id=(me, partner),
-            device_id_type=MESH,
+        return remote(
+            part_out.at[g], part_in.at[g], part_send.at[g], part_recv.at[g], (me, partner)
+        )
+
+    def blocks(source, target, count, send, recv):
+        return remote(
+            source.at[pl.ds(0, count)], target.at[pl.ds(0, count)], send, recv, (me, partner)
         )
 
     fetches[0].wait()
@@ -182,12 +173,12 @@
             for i in range(PLANE):
                 target = flip(my_plane, mask, bits) * PLANE + flip(my_seat, i, 2)
                 if mask or i:
-                    id_copy(target, me).start()
+                    id_copy(target).start()
         for mask in masks:
             for i in range(PLANE):
                 target = flip(my_plane, mask, bits) * PLANE + flip(my_seat, i, 2)
                 if mask or i:
-                    query_copy(target, me).start()
+                    query_copy(target, mask).start()
 
     @pl.when(at_inner == 1)
     def _():
@@ -213,9 +204,7 @@
     landed[me] = outgoing[me]
     for fetch in fetches[2:]:
         fetch.wait()
-    for step in range(1, n):
-        other = (me + step) % n
-        id_copy(other, other).wait_recv()
+    blocks(ids, ids, n - 1, id_send, id_recv).wait_recv()
     scale = math.log2(math.e) / math.sqrt(HEAD_WIDTH)
 
     @pl.loop(0, planes)
@@ -226,10 +215,11 @@
 
         @pl.when(mask > 0)
         def _():
-            query_copy(seats[0], seats[0]).wait_recv()
-
-        for i in range(1, PLANE):
-            query_copy(seats[i], seats[i]).wait_recv()
+            blocks(outgoing, landed, PLANE, send_sem, recv_sem.at[mask]).wait_recv()
+
+        @pl.when(mask == 0)
+        def _():
+            blocks(outgoing, landed, PLANE - 1, send_sem, recv_sem.at[0]).wait_recv()
 
         base = plane * PLANE
         spot = lax.broadcasted_iota(jnp.int32, (capacity, 1), 0).astype(jnp.float32)
@@ -301,27 +291,22 @@
 
         @pl.when(mask > 0)
         def _():
-            back_copy(seats[0], me).start()
+            back_copy(seats[0]).start()
 
         for i in range(1, PLANE):
-            back_copy(seats[i], me).start()
+            back_copy(seats[i]).start()
 
     back[me] = result[me]
-    for step in range(1, n):
-        other = (me + step) % n
-        id_copy(other, me).wait_send()
-        query_copy(other, me).wait_send()
+    blocks(ids, ids, n - 1, id_send, id_recv).wait_send()
+    blocks(outgoing, landed, n - 1, send_sem, recv_sem.at[0]).wait_send()
     for g in range(planes):
         part_copy(g).wait_send()
-    for step in range(1, n):
-        other = (me + step) % n
-        back_copy(other, other).wait_recv()
+    blocks(result, back, n - 1, back_send, back_recv).wait_recv()
     mixed = jnp.dot(
         take[...], back[...].reshape(slots, half), preferred_element_type=jnp.float32
     )
     mixed_ref[...] = mixed.astype(jnp.bfloat16)
-    for step in range(1, n):
-        back_copy((me + step) % n, me).wait_send()
+    blocks(result, back, n - 1, back_send, back_recv).wait_send()
 
 
 def exchange(n, capacity, queries, cached_key_rows, cached_value_rows, parent_ids, lengths, residual, out_weight):
@@ -355,8 +340,7 @@
             held(planes, rows, half),
             pltpu.VMEM((rows, half), jnp.float32),
             held(children, n * capacity),
-            dma((6,)), dma((n,)), dma((n,)), dma((n,)), dma((n,)),
-            dma((planes,)), dma((planes,)), dma((n,)), dma((n,)),
+            dma((6,)), dma, dma, dma, dma((planes,)), dma((planes,)), dma((planes,)), dma, dma,
         ],
         compiler_params=pltpu.CompilerParams(
             collective_id=0, has_side_effects=True, vmem_limit_bytes=VMEM_MB << 20

time: 41.8 us -> 41 us (0.981)
  Pallas kernels: 40.9 us -> 40.1 us
    pallas_call x1, Pallas kernels: 40.9 us -> 40.1 us  [exchange(): pl.pallas_call(functools.partial(exchange_kernel, n), out_shape=jax.Shape...]
where the time goes in v4:
time: 41 us; the launch traced here: 40.9 us
  Pallas kernels  40.1 us (98%)
  other arithmetic  0.77 us (2%)
    pallas_call x1, Pallas kernels, exchange(): pl.pallas_call(functools.partial(exchange_kernel, n), out_shape=jax.Shape...  40.1 us

profile of v4, /device:TPU:8, one launch (start us, length us, event | category | flops | bytes accessed | tf_op | source)
XLA Modules:
  0.0 40.9 jit_solution(8467853046812950489)
XLA Ops:
  0.0 0.0 copy-start
  0.0 40.1 %shard_map.73 = bf16[128,1024]{1,0:T(8,128)(2,1)S(1)} custom-call(bf16[128,2048]{1,0:T(8,128)(2,1)} %query_hbm.1, bf16[2,1024,512]{2,1,0:T(8,128)(2,1)} %key_hbm.1, bf16[2,1024,512]{2,1,0:T(8,128)(2,1)} %value_hbm.1, s32[1,128]{1,0:T(1,128)} %bitcast.1, s32[2]{0:T(128)} %length_hbm.1, bf16[2048,2048]{1,0:T(8,128)(2,1)} %weight_hbm.1), custom_call_target="tpu_custom_call" | custom-call | tf_op jit(solution)/shard_map/pallas_call | solution.py:323
  40.1 0.0 copy-done
  40.1 0.8 %add_convert_fusion = bf16[128,1024]{1,0:T(8,128)(2,1)} fusion(bf16[128,1024]{1,0:T(8,128)(2,1)S(1)} %shard_map.73, bf16[128,1024]{1,0:T(8,128)(2,1)S(1)} %copy-done), kind=kLoop, calls=%fused_computation | loop fusion | flops 524288 | bytes 786432 | tf_op jit(solution)/shard_map/convert_element_type | solution.py:383
Async XLA Ops:
  0.0 40.1 %copy-start = (bf16[128,1024]{1,0:T(8,128)(2,1)S(1)}, bf16[128,1024]{1,0:T(8,128)(2,1)}, u32[]{:S(2)}) copy-start(bf16[128,1024]{1,0:T(8,128)(2,1)} %param.12) | copy-start | bytes 786436

commit v5 on v4

--- a/solution.py
+++ b/solution.py
@@ -175,7 +175,7 @@
                 if mask or i:
                     id_copy(target).start()
         for mask in masks:
-            for i in range(PLANE):
+            for i in reversed(range(PLANE)):
                 target = flip(my_plane, mask, bits) * PLANE + flip(my_seat, i, 2)
                 if mask or i:
                     query_copy(target, mask).start()
@@ -289,12 +289,12 @@
         total = (own[...] + part_in[g].astype(jnp.float32)).astype(jnp.bfloat16)
         result[pl.ds(base, PLANE)] = total.reshape(PLANE, capacity, half)
 
+        for i in range(PLANE - 1, 0, -1):
+            back_copy(seats[i]).start()
+
         @pl.when(mask > 0)
         def _():
             back_copy(seats[0]).start()
-
-        for i in range(1, PLANE):
-            back_copy(seats[i]).start()
 
     back[me] = result[me]
     blocks(ids, ids, n - 1, id_send, id_recv).wait_send()

time: 41 us -> 39.7 us (0.968)
  Pallas kernels: 40.1 us -> 38.8 us
    pallas_call x1, Pallas kernels: 40.1 us -> 38.8 us  [exchange(): pl.pallas_call(functools.partial(exchange_kernel, n), out_shape=jax.Shape...]
where the time goes in v5:
time: 39.7 us; the launch traced here: 39.6 us
  Pallas kernels  38.8 us (98%)
  other arithmetic  0.77 us (2%)
    pallas_call x1, Pallas kernels, exchange(): pl.pallas_call(functools.partial(exchange_kernel, n), out_shape=jax.Shape...  38.8 us

profile of v5, /device:TPU:8, one launch (start us, length us, event | category | flops | bytes accessed | tf_op | source)
XLA Modules:
  0.0 39.6 jit_solution(6495901492401925000)
XLA Ops:
  0.0 0.0 copy-start
  0.0 38.8 %shard_map.73 = bf16[128,1024]{1,0:T(8,128)(2,1)S(1)} custom-call(bf16[128,2048]{1,0:T(8,128)(2,1)} %query_hbm.1, bf16[2,1024,512]{2,1,0:T(8,128)(2,1)} %key_hbm.1, bf16[2,1024,512]{2,1,0:T(8,128)(2,1)} %value_hbm.1, s32[1,128]{1,0:T(1,128)} %bitcast.1, s32[2]{0:T(128)} %length_hbm.1, bf16[2048,2048]{1,0:T(8,128)(2,1)} %weight_hbm.1), custom_call_target="tpu_custom_call" | custom-call | tf_op jit(solution)/shard_map/pallas_call | solution.py:323
  38.8 0.0 copy-done
  38.8 0.8 %add_convert_fusion = bf16[128,1024]{1,0:T(8,128)(2,1)} fusion(bf16[128,1024]{1,0:T(8,128)(2,1)S(1)} %shard_map.73, bf16[128,1024]{1,0:T(8,128)(2,1)S(1)} %copy-done), kind=kLoop, calls=%fused_computation | loop fusion | flops 524288 | bytes 786432 | tf_op jit(solution)/shard_map/convert_element_type | solution.py:383
Async XLA Ops:
  0.0 38.8 %copy-start = (bf16[128,1024]{1,0:T(8,128)(2,1)S(1)}, bf16[128,1024]{1,0:T(8,128)(2,1)}, u32[]{:S(2)}) copy-start(bf16[128,1024]{1,0:T(8,128)(2,1)} %param.12) | copy-start | bytes 786436
